TPU v7x, 256 devices: a whole 4x4x8 slice. The times are simulated.
256 devices in a mesh: row: 32 (over x, z_lo, core), col: 8 (over z_hi, y).
Axes of the slice: x: 4, y: 4, z: 8 (z_hi: 2, z_lo: 4; z = z_hi * 4 + z_lo), core: 2. Of those that a mesh axis runs over, the one named last changes fastest.
Arguments:
- embed_first: bfloat16 [1536, 16384], P('col', 'row'), may hold values from -6 to 6
- embed_second: bfloat16 [1536, 16384], P('row', 'col'), may hold values from -6 to 6
- corr_grad: float32 [16384, 16384], P('row', 'col'), may hold values from -0.046875 to 0.046875
Outputs:
- grad_first: bfloat16 [1536, 16384], P('col', 'row')
- grad_second: bfloat16 [1536, 16384], P('row', 'col')
All inputs are finite; a program needn't handle non-finite values.
Results may differ from a plain program's by a relative error of at most 0.0065.
Values may be sent and summed in bfloat16 or wider, within the bound.
A program may use at most 128 MiB of HBM per device.

v0:
```python
import jax
import jax.numpy as jnp
from jax import lax
from jax.sharding import PartitionSpec as P


def cut_along(x, dim, peers):
    lengths = x.shape
    parts = x.reshape(*lengths[:dim], peers, lengths[dim] // peers, *lengths[dim + 1 :])
    return jnp.moveaxis(parts, dim, 0)


def sent_and_summed(x, axis, dim):
    peers = lax.axis_size(axis)
    parts = lax.all_to_all(cut_along(x, dim, peers), axis, 0, 0, tiled=True)
    return jnp.sum(parts.astype(jnp.float32), axis=0)


def local(embed_first, embed_second, corr_grad):
    low_grad = corr_grad.astype(jnp.bfloat16)
    first_terms = lax.dot_general(
        lax.all_gather(embed_second, "row", axis=0, tiled=True),
        low_grad,
        (((1,), (1,)), ((), ())),
        preferred_element_type=jnp.float32,
    )
    grad_first = sent_and_summed(first_terms.astype(jnp.bfloat16), "col", 0).astype(jnp.bfloat16)
    whole_first = lax.all_gather(embed_first, "col", axis=0, tiled=True)
    grad_second = sent_and_summed(
        jnp.dot(whole_first, low_grad, preferred_element_type=jnp.float32).astype(jnp.bfloat16),
        "row",
        0,
    ).astype(jnp.bfloat16)
    return (grad_first, grad_second)


def solution(mesh):
    return jax.shard_map(
        local,
        mesh=mesh,
        in_specs=(P("col", "row"), P("row", "col"), P("row", "col")),
        out_specs=(P("col", "row"), P("row", "col")),
        check_vma=False,
    )
```

profile of v0, /device:TPU:32, one launch (start us, length us, event | category | flops | bytes accessed | tf_op | source)
XLA Modules:
  0.0 311.2 jit_solution(858558997219356227)
XLA Ops:
  7.2 0.0 all-gather.5.cloned.1.call-start
  7.2 0.7 all-gather.5.cloned.1.call-update
  7.9 0.0 all-gather.3.cloned.1.call-start
  7.9 0.7 all-gather.3.cloned.1.call-update
  8.6 72.8 %all-gather.5.cloned.1.call-done = bf16[1536,512]{1,0:T(8,128)(2,1)} async-done(((bf16[192,512]{1,0:T(8,128)(2,1)}), bf16[1536,512]{1,0:T(8,128)(2,1)}) %all-gather.5.cloned.1.call-update) | async-done | bytes 1572880 | tf_op jit(solution)/shard_map/all_gather | solution.py:28
  81.4 8.8 %convolution_convert_fusion = bf16[1536,2048]{1,0:T(8,128)(2,1)} fusion(bf16[1536,512]{1,0:T(8,128)(2,1)} %all-gather.5.cloned.1.call-done, f32[512,2048]{1,0:T(8,128)} %param.5), kind=kOutput, calls=%fused_computation | convolution fusion | flops 3225419776 | bytes 12058624 | tf_op jit(solution)/shard_map/dot_general | solution.py:30
  90.2 6.0 %all-to-all-start.1 = ((bf16[32,48,2048]{2,1,0:T(8,128)(2,1)}), bf16[32,48,2048]{2,1,0:T(8,128)(2,1)}, u32[]{:S(2)}, u32[]{:S(2)}) async-start(bf16[32,48,2048]{2,1,0:T(8,128)(2,1)} %bitcast.4), calls=%async_computation.1 | async-start | bytes 12582912 | tf_op jit(solution)/shard_map/all_to_all | solution.py:15
  96.2 134.9 %all-gather.3.cloned.1.call-done = bf16[1536,2048]{1,0:T(8,128)(2,1)} async-done(((bf16[48,2048]{1,0:T(8,128)(2,1)}), bf16[1536,2048]{1,0:T(8,128)(2,1)}) %all-gather.3.cloned.1.call-update) | async-done | bytes 6291472 | tf_op jit(solution)/shard_map/all_gather | solution.py:22
  231.1 8.6 %convolution_convert_fusion.1 = bf16[1536,512]{1,0:T(8,128)(2,1)} fusion(bf16[1536,2048]{1,0:T(8,128)(2,1)} %all-gather.3.cloned.1.call-done, f32[512,2048]{1,0:T(8,128)} %param.5), kind=kOutput, calls=%fused_computation.1 | convolution fusion | flops 3223060480 | bytes 12058624 | tf_op jit(solution)/shard_map/dot_general | solution.py:21
  239.8 28.2 %all-to-all-done.1 = bf16[32,48,2048]{2,1,0:T(8,128)(2,1)} async-done(((bf16[32,48,2048]{2,1,0:T(8,128)(2,1)}), bf16[32,48,2048]{2,1,0:T(8,128)(2,1)}, u32[]{:S(2)}, u32[]{:S(2)}) %all-to-all-start.1) | async-done | bytes 6291488 | tf_op jit(solution)/shard_map/all_to_all | solution.py:15
  268.0 7.1 %all-to-all-start = ((bf16[8,192,512]{2,1,0:T(8,128)(2,1)}), bf16[8,192,512]{2,1,0:T(8,128)(2,1)S(1)}, u32[]{:S(2)}, u32[]{:S(2)}) async-start(bf16[8,192,512]{2,1,0:T(8,128)(2,1)} %bitcast), calls=%async_computation | async-start | bytes 3145728 | tf_op jit(solution)/shard_map/all_to_all | solution.py:15
  275.1 4.9 %reduce_sum.25 = bf16[48,2048]{1,0:T(8,128)(2,1)} reduce(bf16[32,48,2048]{2,1,0:T(8,128)(2,1)} %all-to-all-done.1, bf16[]{:T(256)} %constant.3.clone.1), dimensions={0}, to_apply=%region_1.0 | reduce | flops 3047424 | bytes 6488066 | tf_op jit(solution)/shard_map/reduce_sum | solution.py:16
  280.0 23.5 %all-to-all-done = bf16[8,192,512]{2,1,0:T(8,128)(2,1)S(1)} async-done(((bf16[8,192,512]{2,1,0:T(8,128)(2,1)}), bf16[8,192,512]{2,1,0:T(8,128)(2,1)S(1)}, u32[]{:S(2)}, u32[]{:S(2)}) %all-to-all-start) | async-done | bytes 1572896 | tf_op jit(solution)/shard_map/all_to_all | solution.py:15
  303.4 0.9 reduce_sum.24
Async XLA Ops:
  7.2 74.3 %all-gather.5.cloned.1.call-start = ((), (), s32[]{:S(2)}) async-start(), calls=%async_computation.3 | async-start | bytes 1769472 | tf_op jit(solution)/shard_map/all_gather | solution.py:28
  7.9 223.2 %all-gather.3.cloned.1.call-start = ((), (), s32[]{:S(2)}) async-start(), calls=%async_computation.2 | async-start | bytes 6488064 | tf_op jit(solution)/shard_map/all_gather | solution.py:22
  90.2 177.8 %all-to-all-start.1 = ((bf16[32,48,2048]{2,1,0:T(8,128)(2,1)}), bf16[32,48,2048]{2,1,0:T(8,128)(2,1)}, u32[]{:S(2)}, u32[]{:S(2)}) async-start(bf16[32,48,2048]{2,1,0:T(8,128)(2,1)} %bitcast.4), calls=%async_computation.1 | async-start | bytes 12582912 | tf_op jit(solution)/shard_map/all_to_all | solution.py:15
  268.0 35.5 %all-to-all-start = ((bf16[8,192,512]{2,1,0:T(8,128)(2,1)}), bf16[8,192,512]{2,1,0:T(8,128)(2,1)S(1)}, u32[]{:S(2)}, u32[]{:S(2)}) async-start(bf16[8,192,512]{2,1,0:T(8,128)(2,1)} %bitcast), calls=%async_computation | async-start | bytes 3145728 | tf_op jit(solution)/shard_map/all_to_all | solution.py:15
Sparse Core Ops, SparseCore 0:
  10.6 70.8 all-gather.4
  83.3 147.7 all-gather.2
where the time goes:
time: 316 us; the launch traced here: 311 us
  waiting for transfers between devices  261 us (83%)
  matrix products  17.4 us (6%)
  between operations  14 us (4%)
  starting transfers between devices  13.1 us (4%)
  other arithmetic  5.84 us (2%)
    all_gather x1, waiting for transfers between devices, local(): lax.all_gather(embed_second, 'row', axis=0, tiled=True)  135 us
    all_gather x1, waiting for transfers between devices, local(): whole_first = lax.all_gather(embed_first, 'col', axis=0, tiled=True)  72.8 us
    all_to_all x2, waiting for transfers between devices, sent_and_summed(): parts = lax.all_to_all(cut_along(x, dim, peers), axis, 0, 0, tiled=True)  51.7 us
    all_to_all x2, starting transfers between devices, sent_and_summed(): parts = lax.all_to_all(cut_along(x, dim, peers), axis, 0, 0, tiled=True)  13.1 us
    dot_general x1, matrix products, local(): jnp.dot(whole_first, low_grad, preferred_element_type=jnp.float32)  8.75 us
    dot_general x1, matrix products, local(): lax.dot_general(lax.all_gather(embed_second, 'row', axis=0, tiled=True),...  8.64 us
  transfers between devices with their start and end apart: 4, of which 4 were waited for; matrix products, arithmetic and copies ran while one was open for 7% of the time, Pallas kernels for 0%

commit v1 on v0

v1 whole, which is shorter than its diff:
```python
import jax
import jax.numpy as jnp
from jax import lax
from jax.experimental import pallas as pl
from jax.experimental.pallas import tpu as pltpu
from jax.sharding import PartitionSpec as P

BF = jnp.bfloat16
F32 = jnp.float32
MESH = pl.DeviceIdType.MESH


def kernel(e1_hbm, e2_hbm, g_hbm, gf_ref, gs_ref,
           e1s, E1, E2, gst, G, PS, PF, XA, XB, YA, YB, ZO, ZI, SZ, TZ, ZH, FS, FX,
           lsem, gsem, cs, cr, es, er, zs, zr, ys, yr, xs, xr, ps, pr, fs, fr, ss, sr):
    row = lax.axis_index("row")
    col = lax.axis_index("col")
    x, p, c = row // 8, (row // 2) % 4, row % 2
    zh, y = col // 4, col % 4
    s = 1 - 2 * (p // 2)
    mid = ((p + 1) // 2) % 2
    first = p // 2

    def dev(x_=x, p_=p, c_=c, zh_=zh, y_=y):
        return ((x_ * 4 + p_) * 2 + c_, zh_ * 4 + y_)

    xp, xm, xo = (x + 1) % 4, (x + 3) % 4, (x + 2) % 4
    yp, ym, yo = (y + 1) % 4, (y + 3) % 4, (y + 2) % 4
    d_core = dev(c_=1 - c)
    d_xp, d_xm = dev(x_=xp), dev(x_=xm)
    d_yp, d_ym = dev(y_=yp), dev(y_=ym)
    d_zh = dev(zh_=1 - zh)
    d_in = dev(p_=p + s)
    d_out = dev(p_=(p - s + 4) % 4)

    pending, block_sends = [], []

    def rc(src, dst, ssem, rsem, d):
        return pltpu.make_async_remote_copy(src, dst, ssem, rsem, device_id=d, device_id_type=MESH)

    def go(src, dst, ssem, rsem, d):
        cp = rc(src, dst, ssem, rsem, d)
        cp.start()
        pending.append(cp)

    def go_if(when, src, dst, sems, i, rsem, d):
        rc(src, dst, sems.at[i], rsem, d).start()
        block_sends.append((when, sems, i))

    def got(dst, rsem):
        rc(dst, dst, rsem, rsem, d_core).wait_recv()

    o = [p + s * (mid * m + (1 - mid) * e) for m, e in ((0, 0), (-1, 1), (1, 2), (2, 3))]
    t = [p + s * (mid * m + (1 - mid) * e) for m, e in ((2, 3), (1, 2), (-1, 1), (0, 0))]

    l2 = [pltpu.make_async_copy(e2_hbm.at[:, pl.ds(h * 1024, 1024)], E2.at[p, x, h], lsem.at[h]) for h in range(2)]
    l1 = pltpu.make_async_copy(e1_hbm, e1s, lsem.at[2])
    l1own = pltpu.make_async_copy(e1_hbm.at[:, c], E1.at[col, c], lsem.at[3])
    for cp in l2:
        cp.start()
    l1.start()
    l1own.start()
    lg = [pltpu.make_async_copy(g_hbm.at[pl.ds(i * 128, 128)], gst.at[i], gsem.at[i]) for i in range(4)]
    for cp in lg:
        cp.start()

    barrier = pltpu.get_barrier_semaphore()
    for d in (d_core, d_xp, d_xm, d_yp, d_ym, d_zh, d_in):
        pl.semaphore_signal(barrier, 1, device_id=d, device_id_type=MESH)

    @pl.when(mid == 1)
    def _():
        pl.semaphore_signal(barrier, 1, device_id=d_out, device_id_type=MESH)

    pl.semaphore_wait(barrier, 7 + mid)

    for cp in l2:
        cp.wait()

    @pl.when(mid == 1)
    def _():
        go_if(1, E2.at[p, x], E2.at[p, x], zs, 0, zr.at[0], d_in)
        go_if(1, E2.at[p, x], E2.at[p, x], zs, 1, zr.at[0], d_out)

    @pl.when(mid == 0)
    def _():
        go_if(0, E2.at[p, x], E2.at[p, x], zs, 0, zr.at[3], d_in)

    def x_full(k):
        go(E2.at[o[k], x], E2.at[o[k], x], xs.at[k, 0], xr.at[k, 0], d_xp)
        go(E2.at[o[k], x], E2.at[o[k], x], xs.at[k, 1], xr.at[k, 1], d_xm)

    def x_half(k):
        got(E2.at[o[k], xm], xr.at[k, 0])
        go(E2.at[o[k], xm, 0], E2.at[o[k], xm, 0], xs.at[k, 2], xr.at[k, 2], d_xp)
        got(E2.at[o[k], xp], xr.at[k, 1])
        go(E2.at[o[k], xp, 1], E2.at[o[k], xp, 1], xs.at[k, 3], xr.at[k, 3], d_xm)

    def x_end(k):
        got(E2.at[o[k], xo, 0], xr.at[k, 2])
        got(E2.at[o[k], xo, 1], xr.at[k, 3])

    zslot = [None] + [mid * m + (1 - mid) * e for m, e in ((3, 0), (0, 1), (1, 2))]

    def z_step(k):
        got(E2.at[o[k], x], zr.at[zslot[k]])
        x_full(k)

        @pl.when(mid == 1)
        def _():
            d = d_in if k == 1 else d_out
            slot = 1 if k < 3 else 2
            go_if(1, E2.at[o[k], x], E2.at[o[k], x], zs, k + 1, zr.at[slot], d)

    x_full(0)

    l1.wait()
    go(e1s.at[:, 1 - c], E1.at[col, c], cs.at[0], cr.at[0], d_core)
    l1own.wait()
    got(E1.at[col, 1 - c], cr.at[0])

    def y_full(i, q):
        go(E1.at[q * 4 + y], E1.at[q * 4 + y], ys.at[i, 0], yr.at[i, 0], d_yp)
        go(E1.at[q * 4 + y], E1.at[q * 4 + y], ys.at[i, 1], yr.at[i, 1], d_ym)

    def y_half(i, q):
        got(E1.at[q * 4 + ym], yr.at[i, 0])
        go(E1.at[q * 4 + ym, 0], E1.at[q * 4 + ym, 0], ys.at[i, 2], yr.at[i, 2], d_yp)
        got(E1.at[q * 4 + yp], yr.at[i, 1])
        go(E1.at[q * 4 + yp, 1], E1.at[q * 4 + yp, 1], ys.at[i, 3], yr.at[i, 3], d_ym)

    def y_end(i, q):
        got(E1.at[q * 4 + yo, 0], yr.at[i, 2])
        got(E1.at[q * 4 + yo, 1], yr.at[i, 3])

    y_full(0, zh)
    go(E1.at[col], E1.at[col], es.at[0], er.at[0], d_zh)

    for i in range(4):
        lg[i].wait()
        G[c, pl.ds(i * 128, 128), :] = gst[i].astype(BF)
        go(G.at[c, pl.ds(i * 128, 128)], G.at[c, pl.ds(i * 128, 128)], cs.at[1 + i], cr.at[1 + i], d_core)

    def gf_task(a):
        def body(j, carry):
            h, i = j // 2, j % 2
            acc = None
            for hj in range(2):
                lhs = E2[2 * a + i, :, hj].reshape(192, 1024)
                r = lax.dot_general(lhs, G[h, :, pl.ds(hj * 1024, 1024)], (((1,), (1,)), ((), ())),
                                    preferred_element_type=F32)
                acc = r if acc is None else acc + r
            acc = acc.astype(BF).reshape(4, 48, 512)
            for k in range(4):
                PF[2 * k + a, h, i] = acc[k]
            return carry
        lax.fori_loop(0, 4, body, 0)

    def gs_task(xx):
        def body(n, carry):
            acc = None
            for h in range(2):
                lhs = E1[pl.ds(2 * xx, 2), h].reshape(192, 512)
                r = jnp.dot(lhs, G[h, :, pl.ds(pl.multiple_of(n * 512, 512), 512)], preferred_element_type=F32)
                acc = r if acc is None else acc + r
            PS[xx, :, n // 2, :, pl.ds(pl.multiple_of((n % 2) * 512, 512), 512)] = acc.astype(BF).reshape(4, 48, 512)
            return carry
        lax.fori_loop(0, 4, body, 0)

    z_step(1)
    x_half(0)
    y_half(0, zh)
    z_step(2)
    x_half(1)
    for i in range(4):
        got(G.at[1 - c, pl.ds(i * 128, 128)], cr.at[1 + i])
    z_step(3)
    got(E1.at[(1 - zh) * 4 + y], er.at[0])
    y_full(1, 1 - zh)
    x_end(0)
    x_end(1)
    gf_task(first)
    x_half(2)
    y_half(1, 1 - zh)
    y_end(0, zh)
    y_end(1, 1 - zh)
    gs_task(xo)
    x_half(3)

    def xa(k):
        go(PS.at[xo, t[k], 0], XA.at[k, 0], ps.at[k, 0], pr.at[k, 0], d_xp)
        go(PS.at[xo, t[k], 1], XA.at[k, 1], ps.at[k, 1], pr.at[k, 1], d_xm)

    def xb(k):
        got(XA.at[k, 0], pr.at[k, 0])
        PS[xp, t[k], 0] = (PS[xp, t[k], 0].astype(F32) + XA[k, 0].astype(F32)).astype(BF)
        go(PS.at[xp, t[k]], XB.at[k, 0], ps.at[k, 2], pr.at[k, 2], d_xp)
        got(XA.at[k, 1], pr.at[k, 1])
        PS[xm, t[k], 1] = (PS[xm, t[k], 1].astype(F32) + XA[k, 1].astype(F32)).astype(BF)
        go(PS.at[xm, t[k]], XB.at[k, 1], ps.at[k, 3], pr.at[k, 3], d_xm)

    def x_got(k):
        got(XB.at[k, 0], pr.at[k, 2])
        got(XB.at[k, 1], pr.at[k, 3])

    def x_sum(k):
        return PS[x, t[k]].astype(F32) + XB[k, 0].astype(F32) + XB[k, 1].astype(F32)

    def ya(i, q):
        go(PF.at[q * 4 + yo, 0], YA.at[i, 0], fs.at[i, 0], fr.at[i, 0], d_yp)
        go(PF.at[q * 4 + yo, 1], YA.at[i, 1], fs.at[i, 1], fr.at[i, 1], d_ym)

    def yb(i, q):
        got(YA.at[i, 0], fr.at[i, 0])
        PF[q * 4 + yp, 0] = (PF[q * 4 + yp, 0].astype(F32) + YA[i, 0].astype(F32)).astype(BF)
        go(PF.at[q * 4 + yp], YB.at[i, 0], fs.at[i, 2], fr.at[i, 2], d_yp)
        got(YA.at[i, 1], fr.at[i, 1])
        PF[q * 4 + ym, 1] = (PF[q * 4 + ym, 1].astype(F32) + YA[i, 1].astype(F32)).astype(BF)
        go(PF.at[q * 4 + ym], YB.at[i, 1], fs.at[i, 3], fr.at[i, 3], d_ym)

    def y_sum(i, q):
        got(YB.at[i, 0], fr.at[i, 2])
        got(YB.at[i, 1], fr.at[i, 3])
        return PF[q * 4 + y].astype(F32) + YB[i, 0].astype(F32) + YB[i, 1].astype(F32)

    def z_end(k):
        @pl.when(mid == 0)
        def _():
            SZ[k] = x_sum(k).astype(BF)
            go_if(0, SZ.at[k], ZO.at[2 - k], ss, k, sr.at[2 - k], d_in)

    def z_mid(k):
        @pl.when(mid == 1)
        def _():
            buf, slot = ((ZO.at[2], 2), (ZO.at[1], 1), (ZI.at[1], 4))[k]
            got(buf, sr.at[slot])
            SZ[k] = (x_sum(k) + buf[...].astype(F32)).astype(BF)
            to, d = ((1, d_in), (0, d_in), (0, d_out))[k]
            go_if(1, SZ.at[k], ZI.at[to], ss, k, sr.at[3 + to], d)

    xa(0)
    xa(1)
    gs_task(xp)
    gs_task(xm)
    x_end(2)
    x_end(3)
    gf_task(1 - first)
    ya(0, 1 - zh)
    ya(1, zh)
    xb(0)
    xa(2)
    yb(0, 1 - zh)
    xb(1)
    xa(3)
    gs_task(x)
    yb(1, zh)
    x_got(0)
    z_end(0)
    TZ[...] = y_sum(0, 1 - zh).astype(BF)
    go(TZ, ZH, es.at[1], er.at[1], d_zh)
    xb(2)
    z_mid(0)
    x_got(1)
    z_end(1)
    xb(3)
    z_mid(1)
    own = y_sum(1, zh)
    got(ZH, er.at[1])
    FS[...] = (own + ZH[...].astype(F32)).astype(BF)
    go(FS.at[1 - c], FX, cs.at[5], cr.at[5], d_core)
    gf_ref[:, c] = FS[c]
    x_got(2)
    z_end(2)
    z_mid(2)
    got(FX, cr.at[5])
    gf_ref[:, 1 - c] = FX[...]
    x_got(3)
    got(ZI.at[0], sr.at[3])

    @pl.when(mid == 0)
    def _():
        r = (x_sum(3) + ZI[0].astype(F32)).astype(BF)
        gs_ref[:, pl.ds(0, 1024)] = r[0]
        gs_ref[:, pl.ds(1024, 1024)] = r[1]

    @pl.when(mid == 1)
    def _():
        got(ZO.at[0], sr.at[0])
        r = (x_sum(3) + ZI[0].astype(F32) + ZO[0].astype(F32)).astype(BF)
        gs_ref[:, pl.ds(0, 1024)] = r[0]
        gs_ref[:, pl.ds(1024, 1024)] = r[1]

    for cp in pending:
        cp.wait_send()
    for w in (0, 1):
        @pl.when(mid == w)
        def _():
            for when, sems, i in block_sends:
                if when == w:
                    rc(SZ.at[0], SZ.at[0], sems.at[i], sr.at[0], d_core).wait_send()


def local(embed_first, embed_second, corr_grad):
    dma = pltpu.SemaphoreType.DMA
    vm = pltpu.VMEM
    gf, gs = pl.pallas_call(
        kernel,
        out_shape=(jax.ShapeDtypeStruct((2, 2, 48, 512), BF), jax.ShapeDtypeStruct((48, 2048), BF)),
        in_specs=[pl.BlockSpec(memory_space=pl.ANY)] * 3,
        out_specs=[pl.BlockSpec(memory_space=pltpu.VMEM)] * 2,
        scratch_shapes=[
            vm((2, 2, 48, 512), BF),
            vm((8, 2, 2, 48, 512), BF),
            vm((4, 4, 2, 48, 1024), BF),
            vm((4, 128, 2048), F32),
            vm((2, 512, 2048), BF),
            vm((4, 4, 2, 48, 1024), BF),
            vm((8, 2, 2, 48, 512), BF),
            vm((4, 2, 48, 1024), BF),
            vm((4, 2, 2, 48, 1024), BF),
            vm((2, 2, 2, 48, 512), BF),
            vm((2, 2, 2, 2, 48, 512), BF),
            vm((3, 2, 48, 1024), BF),
            vm((2, 2, 48, 1024), BF),
            vm((3, 2, 48, 1024), BF),
            vm((2, 2, 48, 512), BF),
            vm((2, 2, 48, 512), BF),
            vm((2, 2, 48, 512), BF),
            vm((2, 48, 512), BF),
            dma((4,)), dma((4,)),
            dma((6,)), dma((6,)),
            dma((2,)), dma((2,)),
            dma((5,)), dma((4,)),
            dma((2, 4)), dma((2, 4)),
            dma((4, 4)), dma((4, 4)),
            dma((4, 4)), dma((4, 4)),
            dma((2, 4)), dma((2, 4)),
            dma((3,)), dma((5,)),
        ],
        compiler_params=pltpu.CompilerParams(
            collective_id=0, has_side_effects=True, vmem_limit_bytes=60 * 2**20
        ),
    )(embed_first.reshape(2, 2, 48, 512), embed_second, corr_grad)
    return gf.reshape(192, 512), gs


def solution(mesh):
    return jax.shard_map(
        local,
        mesh=mesh,
        in_specs=(P("col", "row"), P("row", "col"), P("row", "col")),
        out_specs=(P("col", "row"), P("row", "col")),
        check_vma=False,
    )
```

time: 316 us -> 86.7 us (0.27)
  the two profiles are of different devices: /device:TPU:32 before, /device:TPU:8 now
where the time goes in v1:
time: 86.7 us; the launch traced here: 86.5 us
  Pallas kernels  82.7 us (95%)
  local copies, waits for them, and re-layouts  3.23 us (4%)
    pallas_call x1, Pallas kernels, local(): pl.pallas_call(kernel, out_shape=(jax.ShapeDtypeStruct((2, 2, 48, 512), B...  82.7 us
    unnamed x2, local copies, waits for them, and re-layouts  3.23 us

profile of v1, /device:TPU:8, one launch (start us, length us, event | category | flops | bytes accessed | tf_op | source)
XLA Modules:
  0.0 86.5 jit_solution(11310896680547716985)
XLA Ops:
  0.6 82.7 %shard_map.50 = (bf16[2,2,48,512]{3,2,1,0:T(8,128)(2,1)}, bf16[48,2048]{1,0:T(8,128)(2,1)}) custom-call(bf16[2,2,48,512]{3,2,1,0:T(8,128)(2,1)} %bitcast.2, bf16[48,2048]{1,0:T(8,128)(2,1)} %e2_hbm.1, f32[512,2048]{1,0:T(8,128)} %g_hbm.1), custom_call_target="tpu_custom_call" | custom-call | tf_op jit(solution)/shard_map/pallas_call | solution.py:306
  83.3 1.6 %copy.7 = bf16[192,512]{1,0:T(8,128)(2,1)} copy(bf16[192,512]{1,0:T(8,128)(2,1)} %bitcast.3) | data formatting | bytes 393216
  84.9 1.6 %copy.8 = bf16[48,2048]{1,0:T(8,128)(2,1)} copy(bf16[48,2048]{1,0:T(8,128)(2,1)} %get-tuple-element.9) | data formatting | bytes 393216

commit v2 on v0

v2 whole, which is shorter than its diff:
```python
import jax
import jax.numpy as jnp
from jax import lax
from jax.experimental import pallas as pl
from jax.experimental.pallas import tpu as pltpu
from jax.sharding import PartitionSpec as P

BF = jnp.bfloat16
F32 = jnp.float32
MESH = pl.DeviceIdType.MESH


def kernel(e1_hbm, e2_hbm, g_hbm, gf_ref, gs_ref,
           e1s, E1, E2, gst, G, PS, PF, XA, XB, YA, YB, ZO, ZI, SZ, TZ, ZH, FS, FX,
           lsem, gsem, cs, cr, es, er, zs, zr, ys, yr, xs, xr, ps, pr, fs, fr, ss, sr):
    row = lax.axis_index("row")
    col = lax.axis_index("col")
    x, p, c = row // 8, (row // 2) % 4, row % 2
    zh, y = col // 4, col % 4
    s = 1 - 2 * (p // 2)
    mid = ((p + 1) // 2) % 2
    first = p // 2

    def dev(x_=x, p_=p, c_=c, zh_=zh, y_=y):
        return ((x_ * 4 + p_) * 2 + c_, zh_ * 4 + y_)

    xp, xm, xo = (x + 1) % 4, (x + 3) % 4, (x + 2) % 4
    yp, ym, yo = (y + 1) % 4, (y + 3) % 4, (y + 2) % 4
    d_core = dev(c_=1 - c)
    d_xp, d_xm = dev(x_=xp), dev(x_=xm)
    d_yp, d_ym = dev(y_=yp), dev(y_=ym)
    d_zh = dev(zh_=1 - zh)
    d_in = dev(p_=p + s)
    d_out = dev(p_=(p - s + 4) % 4)

    sends, side = [], [0]

    def rc(src, dst, ssem, rsem, d):
        return pltpu.make_async_remote_copy(src, dst, ssem, rsem, device_id=d, device_id_type=MESH)

    def go(src, dst, sems, i, rsem, d):
        go_if(None, src, dst, sems, i, rsem, d)

    def go_if(when, src, dst, sems, i, rsem, d):
        rc(src, dst, sems.at[i], rsem, d).start()
        if not any(w == when and a is sems and b == i for w, a, b in sends):
            sends.append((when, sems, i))

    def got(dst, rsem):
        rc(dst, dst, rsem, rsem, d_core).wait_recv()

    o = [p + s * (mid * m + (1 - mid) * e) for m, e in ((0, 0), (-1, 1), (1, 2), (2, 3))]
    t = [p + s * (mid * m + (1 - mid) * e) for m, e in ((2, 3), (1, 2), (-1, 1), (0, 0))]

    l2 = [pltpu.make_async_copy(e2_hbm.at[:, pl.ds(h * 1024, 1024)], E2.at[p, x, h], lsem.at[h]) for h in range(2)]
    l1 = pltpu.make_async_copy(e1_hbm, e1s, lsem.at[2])
    l1own = pltpu.make_async_copy(e1_hbm.at[:, c], E1.at[col, c], lsem.at[3])
    for cp in l2:
        cp.start()
    l1.start()
    l1own.start()
    lg = [pltpu.make_async_copy(g_hbm.at[pl.ds(i * 128, 128)], gst.at[i], gsem.at[i]) for i in range(4)]
    for cp in lg:
        cp.start()

    barrier = pltpu.get_barrier_semaphore()
    for d in (d_core, d_xp, d_xm, d_yp, d_ym, d_zh, d_in):
        pl.semaphore_signal(barrier, 1, device_id=d, device_id_type=MESH)

    @pl.when(mid == 1)
    def _():
        pl.semaphore_signal(barrier, 1, device_id=d_out, device_id_type=MESH)

    pl.semaphore_wait(barrier, 7 + mid)

    for cp in l2:
        cp.wait()

    @pl.when(mid == 1)
    def _():
        for h in range(2):
            go_if(1, E2.at[p, x, h], E2.at[p, x, h], zs, (0, h), zr.at[0, h], d_in)
            go_if(1, E2.at[p, x, h], E2.at[p, x, h], zs, (1, h), zr.at[0, h], d_out)

    @pl.when(mid == 0)
    def _():
        for h in range(2):
            go_if(0, E2.at[p, x, h], E2.at[p, x, h], zs, (0, h), zr.at[3, h], d_in)

    def x_send(k, r, h):
        go(E2.at[o[k], x, h], E2.at[o[k], x, h], xs, (k, r, h,), xr.at[k, r, h], (d_xp, d_xm)[r])

    def x_fwd(k):
        for r, frm, to in ((0, xm, d_xp), (1, xp, d_xm)):
            got(E2.at[o[k], frm, r], xr.at[k, r, r])
            go(E2.at[o[k], frm, r], E2.at[o[k], frm, r], xs, (k, 2, r,), xr.at[k, 2, r], to)

    def x_end(k):
        got(E2.at[o[k], xm, 1], xr.at[k, 0, 1])
        got(E2.at[o[k], xp, 0], xr.at[k, 1, 0])
        got(E2.at[o[k], xo, 0], xr.at[k, 2, 0])
        got(E2.at[o[k], xo, 1], xr.at[k, 2, 1])

    zslot = [None] + [mid * m + (1 - mid) * e for m, e in ((3, 0), (0, 1), (1, 2))]

    def z_step(k, h):
        got(E2.at[o[k], x, h], zr.at[zslot[k], h])
        x_send(k, 0, h)
        x_send(k, 1, h)

        if side[0]:
            d = d_in if k == 1 else d_out
            slot = 1 if k < 3 else 2
            go_if(1, E2.at[o[k], x, h], E2.at[o[k], x, h], zs, (k + 1, h), zr.at[slot, h], d)

    for r, h in ((0, 0), (1, 1), (0, 1), (1, 0)):
        x_send(0, r, h)

    l1.wait()
    go(e1s.at[:, 1 - c], E1.at[col, c], cs, (0,), cr.at[0], d_core)
    l1own.wait()
    got(E1.at[col, 1 - c], cr.at[0])

    def y_send(i, q, r, h):
        b = q * 4 + y
        go(E1.at[b, h], E1.at[b, h], ys, (i, r, h,), yr.at[i, r, h], (d_yp, d_ym)[r])

    def y_fwd(i, q):
        for r, frm, to in ((0, q * 4 + ym, d_yp), (1, q * 4 + yp, d_ym)):
            got(E1.at[frm, r], yr.at[i, r, r])
            go(E1.at[frm, r], E1.at[frm, r], ys, (i, 2, r,), yr.at[i, 2, r], to)

    def y_end(i, q):
        got(E1.at[q * 4 + ym, 1], yr.at[i, 0, 1])
        got(E1.at[q * 4 + yp, 0], yr.at[i, 1, 0])
        got(E1.at[q * 4 + yo, 0], yr.at[i, 2, 0])
        got(E1.at[q * 4 + yo, 1], yr.at[i, 2, 1])

    for r, h in ((0, 0), (1, 1), (0, 1), (1, 0)):
        y_send(0, zh, r, h)

    def zh_send():
        for h in range(2):
            go(E1.at[col, h], E1.at[col, h], es, (0, h,), er.at[0, h], d_zh)

    def zh_got(h):
        got(E1.at[(1 - zh) * 4 + y, h], er.at[0, h])
        y_send(1, 1 - zh, 0, h)
        y_send(1, 1 - zh, 1, h)

    for i in range(4):
        lg[i].wait()
        G[c, pl.ds(i * 128, 128), :] = gst[i].astype(BF)
        go(G.at[c, pl.ds(i * 128, 128)], G.at[c, pl.ds(i * 128, 128)], cs, (1 + i,), cr.at[1 + i], d_core)

    def g_got():
        for i in range(4):
            got(G.at[1 - c, pl.ds(i * 128, 128)], cr.at[1 + i])

    def gf_task(k):
        ok = o[k]
        a, i = ok // 2, ok % 2

        def body(h, carry):
            acc = None
            for hj in range(2):
                lhs = E2[ok, :, hj].reshape(192, 1024)
                r = lax.dot_general(lhs, G[h, :, pl.ds(hj * 1024, 1024)], (((1,), (1,)), ((), ())),
                                    preferred_element_type=F32)
                acc = r if acc is None else acc + r
            acc = acc.astype(BF).reshape(4, 48, 512)
            for n in range(4):
                PF[2 * n + a, h, i] = acc[n]
            return carry
        lax.fori_loop(0, 2, body, 0)

    def gs_task(xx):
        def body(n, carry):
            acc = None
            for h in range(2):
                lhs = E1[pl.ds(2 * xx, 2), h].reshape(192, 512)
                r = jnp.dot(lhs, G[h, :, pl.ds(pl.multiple_of(n * 512, 512), 512)], preferred_element_type=F32)
                acc = r if acc is None else acc + r
            PS[xx, :, n // 2, :, pl.ds(pl.multiple_of((n % 2) * 512, 512), 512)] = acc.astype(BF).reshape(4, 48, 512)
            return carry
        lax.fori_loop(0, 4, body, 0)

    def xa(k):
        for r, d in ((0, d_xp), (1, d_xm)):
            go(PS.at[xo, t[k], r], XA.at[k, r], ps, (k, 0, r,), pr.at[k, 0, r], d)

    def xb(k):
        for r, n, d in ((0, xp, d_xp), (1, xm, d_xm)):
            go(PS.at[n, t[k], 1 - r], XB.at[k, r, 1 - r], ps, (k, 1, r,), pr.at[k, 1, r], d)

    def xc(k):
        for r, n, d in ((0, xp, d_xp), (1, xm, d_xm)):
            got(XA.at[k, r], pr.at[k, 0, r])
            PS[n, t[k], r] = (PS[n, t[k], r].astype(F32) + XA[k, r].astype(F32)).astype(BF)
            go(PS.at[n, t[k], r], XB.at[k, r, r], ps, (k, 2, r,), pr.at[k, 2, r], d)

    def x_got(k):
        for r in range(2):
            got(XB.at[k, r, 1 - r], pr.at[k, 1, r])
            got(XB.at[k, r, r], pr.at[k, 2, r])

    def x_sum(k, h):
        return PS[x, t[k], h].astype(F32) + XB[k, 0, h].astype(F32) + XB[k, 1, h].astype(F32)

    def ya(i, q):
        for r, d in ((0, d_yp), (1, d_ym)):
            go(PF.at[q * 4 + yo, r], YA.at[i, r], fs, (i, 0, r,), fr.at[i, 0, r], d)

    def yb(i, q):
        for r, n, d in ((0, yp, d_yp), (1, ym, d_ym)):
            go(PF.at[q * 4 + n, 1 - r], YB.at[i, r, 1 - r], fs, (i, 1, r,), fr.at[i, 1, r], d)

    def yc(i, q):
        for r, n, d in ((0, yp, d_yp), (1, ym, d_ym)):
            got(YA.at[i, r], fr.at[i, 0, r])
            PF[q * 4 + n, r] = (PF[q * 4 + n, r].astype(F32) + YA[i, r].astype(F32)).astype(BF)
            go(PF.at[q * 4 + n, r], YB.at[i, r, r], fs, (i, 2, r,), fr.at[i, 2, r], d)

    def y_sum(i, q):
        for r in range(2):
            got(YB.at[i, r, 1 - r], fr.at[i, 1, r])
            got(YB.at[i, r, r], fr.at[i, 2, r])
        return PF[q * 4 + y].astype(F32) + YB[i, 0].astype(F32) + YB[i, 1].astype(F32)

    def z_end(k):
        for h in range(2):
            SZ[k, h] = x_sum(k, h).astype(BF)
            go_if(0, SZ.at[k, h], ZO.at[2 - k, h], ss, (k, h), sr.at[2 - k, h], d_in)

    def z_mid(k, h):
        buf, slot = ((ZO.at[2], 2), (ZO.at[1], 1), (ZI.at[1], 4))[k]
        got(buf.at[h], sr.at[slot, h])
        SZ[k, h] = (x_sum(k, h) + buf[h].astype(F32)).astype(BF)
        to, d = ((1, d_in), (0, d_in), (0, d_out))[k]
        go_if(1, SZ.at[k, h], ZI.at[to, h], ss, (k, h), sr.at[3 + to, h], d)

    def tz():
        TZ[...] = y_sum(0, 1 - zh).astype(BF)
        for h in range(2):
            go(TZ.at[h], ZH.at[h], es, (1, h,), er.at[1, h], d_zh)

    def own(cl, f, *a):
        @pl.when((y + cl) % 2 == 0)
        def _():
            f(*a)

    def relay(cl, f, *a):
        @pl.when((y + cl) % 2 == 1)
        def _():
            f(*a)

    def gf_end():
        mine = y_sum(1, zh)
        for h in range(2):
            got(ZH.at[h], er.at[1, h])
        FS[...] = (mine + ZH[...].astype(F32)).astype(BF)
        go(FS.at[1 - c], FX, cs, (5,), cr.at[5], d_core)
        gf_ref[:, c] = FS[c]

    def gf_out():
        got(FX, cr.at[5])
        gf_ref[:, 1 - c] = FX[...]

    def gs_out(h):
        got(ZI.at[0, h], sr.at[3, h])

        total = x_sum(3, h) + ZI[0, h].astype(F32)
        if side[0]:
            got(ZO.at[0, h], sr.at[0, h])
            total = total + ZO[0, h].astype(F32)
        gs_ref[:, pl.ds(h * 1024, 1024)] = total.astype(BF)

    early = 2 * zh
    late = 2 * (1 - zh)
    odd = xo % 2

    def run(*steps):
        for f, *a in steps:
            with jax.named_scope(f.__name__ + "_".join(getattr(v, "__name__", str(v)) if isinstance(v, int) or callable(v) else "v" for v in a)):
                f(*a)

    def finish(w):
        for when, sems, i in sends:
            if when is None or when == w:
                like = G.at[0, pl.ds(0, 128)] if sems is cs and 1 <= i[0] <= 4 else SZ.at[0, 0]
                rc(like, like, sems.at[i], sr.at[0, 0], d_core).wait_send()

    @pl.when(mid == 0)
    def _():
        side[0] = 0
        run(
            (zh_send,), (x_fwd, 0), (z_step, 1, 0), (y_fwd, 0, zh), (z_step, 1, 1), (x_fwd, 1), (zh_got, 0),
            (x_end, 0), (g_got,), (gf_task, 0), (zh_got, 1), (y_end, 0, zh), (gs_task, early), (z_step, 2, 0), (z_step, 2, 1),
            (y_fwd, 1, 1 - zh), (x_end, 1), (gf_task, 1), (own, first, ya, 0, 1 - zh), (relay, first, yb, 0, 1 - zh), (own, first, ya, 1, zh),
            (x_fwd, 2), (z_step, 3, 0), (z_step, 3, 1), (gs_task, early + 1),
            (y_end, 1, 1 - zh), (gs_task, late + odd), (xa, 0), (relay, first, yc, 0, 1 - zh), (gs_task, late + 1 - odd),
            (relay, first, yb, 1, zh), (relay, first, yc, 1, zh),
            (x_end, 2), (gf_task, 2), (x_fwd, 3), (xb, 0), (xc, 0), (xa, 1), (xb, 1), (xa, 2), (own, first, tz),
            (x_end, 3), (gf_task, 3), (own, 1 - first, ya, 0, 1 - zh), (relay, 1 - first, yb, 0, 1 - zh), (own, 1 - first, ya, 1, zh),
            (xc, 1), (xb, 2), (xa, 3), (x_got, 0), (z_end, 0),
            (relay, 1 - first, yc, 0, 1 - zh), (relay, 1 - first, yb, 1, zh), (relay, 1 - first, yc, 1, zh),
            (xc, 2), (xb, 3), (own, 1 - first, tz), (x_got, 1), (z_end, 1), (xc, 3),
            (x_got, 2), (z_end, 2), (gf_end,), (gf_out,),
            (x_got, 3), (gs_out, 0), (gs_out, 1),
        )
        finish(0)

    @pl.when(mid == 1)
    def _():
        side[0] = 1
        run(
            (zh_send,), (x_fwd, 0), (z_step, 1, 0), (z_step, 2, 0), (y_fwd, 0, zh), (z_step, 1, 1), (z_step, 2, 1),
            (x_end, 0), (g_got,), (gf_task, 0), (z_step, 3, 0), (zh_got, 0), (z_step, 3, 1), (zh_got, 1), (x_fwd, 1),
            (y_end, 0, zh), (gs_task, early), (x_fwd, 2), (y_fwd, 1, 1 - zh), (x_end, 1), (gf_task, 1),
            (own, first, ya, 0, 1 - zh), (relay, first, yb, 0, 1 - zh), (own, first, ya, 1, zh), (gs_task, early + 1),
            (x_fwd, 3), (y_end, 1, 1 - zh), (gs_task, late + odd), (xa, 0), (relay, first, yc, 0, 1 - zh), (gs_task, late + 1 - odd), (xb, 0),
            (xa, 1), (relay, first, yb, 1, zh), (relay, first, yc, 1, zh),
            (x_end, 2), (gf_task, 2), (xc, 0), (xb, 1), (xa, 2),
            (x_end, 3), (gf_task, 3), (own, 1 - first, ya, 0, 1 - zh), (relay, 1 - first, yb, 0, 1 - zh), (own, 1 - first, ya, 1, zh),
            (own, first, tz),
            (xc, 1), (xb, 2), (xa, 3), (x_got, 0),
            (relay, 1 - first, yc, 0, 1 - zh), (relay, 1 - first, yb, 1, zh), (relay, 1 - first, yc, 1, zh), (xc, 2), (xb, 3),
            (z_mid, 0, 0), (z_mid, 0, 1), (own, 1 - first, tz), (xc, 3), (x_got, 1),
            (z_mid, 1, 0), (z_mid, 1, 1), (x_got, 2), (z_mid, 2, 0), (z_mid, 2, 1), (gf_end,), (gf_out,),
            (x_got, 3), (gs_out, 0), (gs_out, 1),
        )
        finish(1)


def local(embed_first, embed_second, corr_grad):
    dma = pltpu.SemaphoreType.DMA
    vm = pltpu.VMEM
    hbm = lambda a: pltpu.with_memory_space_constraint(a, pltpu.HBM)
    gf, gs = pl.pallas_call(
        kernel,
        out_shape=(jax.ShapeDtypeStruct((2, 2, 48, 512), BF), jax.ShapeDtypeStruct((48, 2048), BF)),
        in_specs=[pl.BlockSpec(memory_space=pl.ANY)] * 3,
        out_specs=[pl.BlockSpec(memory_space=pltpu.VMEM)] * 2,
        scratch_shapes=[
            vm((2, 2, 48, 512), BF),
            vm((8, 2, 2, 48, 512), BF),
            vm((4, 4, 2, 48, 1024), BF),
            vm((4, 128, 2048), F32),
            vm((2, 512, 2048), BF),
            vm((4, 4, 2, 48, 1024), BF),
            vm((8, 2, 2, 48, 512), BF),
            vm((4, 2, 48, 1024), BF),
            vm((4, 2, 2, 48, 1024), BF),
            vm((2, 2, 2, 48, 512), BF),
            vm((2, 2, 2, 2, 48, 512), BF),
            vm((3, 2, 48, 1024), BF),
            vm((2, 2, 48, 1024), BF),
            vm((3, 2, 48, 1024), BF),
            vm((2, 2, 48, 512), BF),
            vm((2, 2, 48, 512), BF),
            vm((2, 2, 48, 512), BF),
            vm((2, 48, 512), BF),
            dma((4,)), dma((4,)),
            dma((6,)), dma((6,)),
            dma((2, 2)), dma((2, 2)),
            dma((5, 2)), dma((4, 2)),
            dma((2, 3, 2)), dma((2, 3, 2)),
            dma((4, 3, 2)), dma((4, 3, 2)),
            dma((4, 3, 2)), dma((4, 3, 2)),
            dma((2, 3, 2)), dma((2, 3, 2)),
            dma((3, 2)), dma((5, 2)),
        ],
        compiler_params=pltpu.CompilerParams(
            collective_id=0, has_side_effects=True, vmem_limit_bytes=50 * 2**20
        ),
    )(hbm(embed_first.reshape(2, 2, 48, 512)), hbm(embed_second), hbm(corr_grad))
    return gf.reshape(192, 512), gs


def solution(mesh):
    return jax.shard_map(
        local,
        mesh=mesh,
        in_specs=(P("col", "row"), P("row", "col"), P("row", "col")),
        out_specs=(P("col", "row"), P("row", "col")),
        check_vma=False,
    )
```

time: 316 us -> 74.8 us (0.24)
  the two profiles are of different devices: /device:TPU:32 before, /device:TPU:8 now
where the time goes in v2:
time: 74.8 us; the launch traced here: 74.7 us
  Pallas kernels  72.7 us (97%)
  local copies, waits for them, and re-layouts  1.36 us (2%)
    pallas_call x1, Pallas kernels, local(): pl.pallas_call(kernel, out_shape=(jax.ShapeDtypeStruct((2, 2, 48, 512), B...  72.7 us

profile of v2, /device:TPU:8, one launch (start us, length us, event | category | flops | bytes accessed | tf_op | source)
XLA Modules:
  0.0 74.7 jit_solution(8843183135774523460)
XLA Ops:
  0.6 72.7 %shard_map.50 = (bf16[2,2,48,512]{3,2,1,0:T(8,128)(2,1)S(1)}, bf16[48,2048]{1,0:T(8,128)(2,1)S(1)}) custom-call(bf16[2,2,48,512]{3,2,1,0:T(8,128)(2,1)} %bitcast.3, bf16[48,2048]{1,0:T(8,128)(2,1)} %e2_hbm.1, f32[512,2048]{1,0:T(8,128)} %g_hbm.1), custom_call_target="tpu_custom_call" | custom-call | tf_op jit(solution)/shard_map/pallas_call | solution.py:339
  73.3 0.7 copy.7
  74.0 0.7 copy.8

commit v3 on v2

--- a/solution.py
+++ b/solution.py
@@ -54,7 +54,7 @@
 
     l2 = [pltpu.make_async_copy(e2_hbm.at[:, pl.ds(h * 1024, 1024)], E2.at[p, x, h], lsem.at[h]) for h in range(2)]
     l1 = pltpu.make_async_copy(e1_hbm, e1s, lsem.at[2])
-    l1own = pltpu.make_async_copy(e1_hbm.at[:, c], E1.at[col, c], lsem.at[3])
+    l1own = pltpu.make_async_copy(e1_hbm.at[:, c], E1.at[col, :, c], lsem.at[3])
     for cp in l2:
         cp.start()
     l1.start()
@@ -103,10 +103,14 @@
 
     zslot = [None] + [mid * m + (1 - mid) * e for m, e in ((3, 0), (0, 1), (1, 2))]
 
-    def z_step(k, h):
-        got(E2.at[o[k], x, h], zr.at[zslot[k], h])
+    def x_out(k, h):
         x_send(k, 0, h)
         x_send(k, 1, h)
+
+    def z_step(k, h, out=1):
+        got(E2.at[o[k], x, h], zr.at[zslot[k], h])
+        if out:
+            x_out(k, h)
 
         if side[0]:
             d = d_in if k == 1 else d_out
@@ -117,34 +121,36 @@
         x_send(0, r, h)
 
     l1.wait()
-    go(e1s.at[:, 1 - c], E1.at[col, c], cs, (0,), cr.at[0], d_core)
+    go(e1s.at[:, 1 - c], E1.at[col, :, c], cs, (0,), cr.at[0], d_core)
     l1own.wait()
-    got(E1.at[col, 1 - c], cr.at[0])
+    got(E1.at[col, :, 1 - c], cr.at[0])
+
+    w0 = (p + 1 + mid) % 2
+    half = (w0, 1 - w0)
 
     def y_send(i, q, r, h):
-        b = q * 4 + y
-        go(E1.at[b, h], E1.at[b, h], ys, (i, r, h,), yr.at[i, r, h], (d_yp, d_ym)[r])
-
-    def y_fwd(i, q):
-        for r, frm, to in ((0, q * 4 + ym, d_yp), (1, q * 4 + yp, d_ym)):
-            got(E1.at[frm, r], yr.at[i, r, r])
-            go(E1.at[frm, r], E1.at[frm, r], ys, (i, 2, r,), yr.at[i, 2, r], to)
-
-    def y_end(i, q):
-        got(E1.at[q * 4 + ym, 1], yr.at[i, 0, 1])
-        got(E1.at[q * 4 + yp, 0], yr.at[i, 1, 0])
-        got(E1.at[q * 4 + yo, 0], yr.at[i, 2, 0])
-        got(E1.at[q * 4 + yo, 1], yr.at[i, 2, 1])
+        b = E1.at[q * 4 + y, half[h]]
+        go(b, b, ys, (i, r, h), yr.at[i, r, h], (d_yp, d_ym)[r])
+
+    def y_fwd(i, q, r):
+        frm, to = ((q * 4 + ym, d_yp), (q * 4 + yp, d_ym))[r]
+        got(E1.at[frm, half[r]], yr.at[i, r, r])
+        go(E1.at[frm, half[r]], E1.at[frm, half[r]], ys, (i, 2, r), yr.at[i, 2, r], to)
+
+    def y_end(i, q, h):
+        got(E1.at[q * 4 + (yp, ym)[h], half[h]], yr.at[i, 1 - h, h])
+        got(E1.at[q * 4 + yo, half[h]], yr.at[i, 2, h])
 
     for r, h in ((0, 0), (1, 1), (0, 1), (1, 0)):
         y_send(0, zh, r, h)
 
-    def zh_send():
-        for h in range(2):
-            go(E1.at[col, h], E1.at[col, h], es, (0, h,), er.at[0, h], d_zh)
+    def zh_send(*hs):
+        for h in hs:
+            b = E1.at[col, half[h]]
+            go(b, b, es, (0, h), er.at[0, h], d_zh)
 
     def zh_got(h):
-        got(E1.at[(1 - zh) * 4 + y, h], er.at[0, h])
+        got(E1.at[(1 - zh) * 4 + y, half[h]], er.at[0, h])
         y_send(1, 1 - zh, 0, h)
         y_send(1, 1 - zh, 1, h)
 
@@ -174,14 +180,16 @@
             return carry
         lax.fori_loop(0, 2, body, 0)
 
-    def gs_task(xx):
+    def gs_task(q, w):
         def body(n, carry):
             acc = None
             for h in range(2):
-                lhs = E1[pl.ds(2 * xx, 2), h].reshape(192, 512)
+                lhs = E1[pl.ds(4 * q, 4), half[w], h].reshape(192, 512)
                 r = jnp.dot(lhs, G[h, :, pl.ds(pl.multiple_of(n * 512, 512), 512)], preferred_element_type=F32)
                 acc = r if acc is None else acc + r
-            PS[xx, :, n // 2, :, pl.ds(pl.multiple_of((n % 2) * 512, 512), 512)] = acc.astype(BF).reshape(4, 48, 512)
+            acc = acc.astype(BF).reshape(4, 48, 512)
+            for j in range(4):
+                PS[2 * q + j // 2, 2 * (j % 2) + half[w], n // 2, :, pl.ds(pl.multiple_of((n % 2) * 512, 512), 512)] = acc[j]
             return carry
         lax.fori_loop(0, 4, body, 0)
 
@@ -275,10 +283,6 @@
             total = total + ZO[0, h].astype(F32)
         gs_ref[:, pl.ds(h * 1024, 1024)] = total.astype(BF)
 
-    early = 2 * zh
-    late = 2 * (1 - zh)
-    odd = xo % 2
-
     def run(*steps):
         for f, *a in steps:
             with jax.named_scope(f.__name__ + "_".join(getattr(v, "__name__", str(v)) if isinstance(v, int) or callable(v) else "v" for v in a)):
@@ -294,18 +298,18 @@
     def _():
         side[0] = 0
         run(
-            (zh_send,), (x_fwd, 0), (z_step, 1, 0), (y_fwd, 0, zh), (z_step, 1, 1), (x_fwd, 1), (zh_got, 0),
-            (x_end, 0), (g_got,), (gf_task, 0), (zh_got, 1), (y_end, 0, zh), (gs_task, early), (z_step, 2, 0), (z_step, 2, 1),
-            (y_fwd, 1, 1 - zh), (x_end, 1), (gf_task, 1), (own, first, ya, 0, 1 - zh), (relay, first, yb, 0, 1 - zh), (own, first, ya, 1, zh),
-            (x_fwd, 2), (z_step, 3, 0), (z_step, 3, 1), (gs_task, early + 1),
-            (y_end, 1, 1 - zh), (gs_task, late + odd), (xa, 0), (relay, first, yc, 0, 1 - zh), (gs_task, late + 1 - odd),
-            (relay, first, yb, 1, zh), (relay, first, yc, 1, zh),
-            (x_end, 2), (gf_task, 2), (x_fwd, 3), (xb, 0), (xc, 0), (xa, 1), (xb, 1), (xa, 2), (own, first, tz),
-            (x_end, 3), (gf_task, 3), (own, 1 - first, ya, 0, 1 - zh), (relay, 1 - first, yb, 0, 1 - zh), (own, 1 - first, ya, 1, zh),
-            (xc, 1), (xb, 2), (xa, 3), (x_got, 0), (z_end, 0),
-            (relay, 1 - first, yc, 0, 1 - zh), (relay, 1 - first, yb, 1, zh), (relay, 1 - first, yc, 1, zh),
-            (xc, 2), (xb, 3), (own, 1 - first, tz), (x_got, 1), (z_end, 1), (xc, 3),
-            (x_got, 2), (z_end, 2), (gf_end,), (gf_out,),
+            (zh_send, 0), (x_fwd, 0), (z_step, 1, 0), (y_fwd, 0, zh, 0), (y_fwd, 0, zh, 1), (z_step, 1, 1), (zh_got, 0),
+            (x_end, 0), (g_got,), (gf_task, 0), (x_fwd, 1), (z_step, 2, 0), (y_end, 0, zh, 0), (gs_task, zh, 0), (z_step, 2, 1), (zh_send, 1),
+            (y_fwd, 1, 1 - zh, 0), (x_end, 1), (gf_task, 1), (own, first, ya, 0, 1 - zh), (relay, first, yb, 0, 1 - zh), (own, first, ya, 1, zh),
+            (z_step, 3, 0), (x_fwd, 2), (z_step, 3, 1), (zh_got, 1), (y_end, 1, 1 - zh, 0), (gs_task, 1 - zh, 0), (xa, 0),
+            (relay, first, yc, 0, 1 - zh), (y_end, 0, zh, 1), (gs_task, zh, 1), (y_fwd, 1, 1 - zh, 1), (relay, first, yb, 1, zh),
+            (x_end, 2), (gf_task, 2), (x_fwd, 3), (xb, 0), (xa, 2), (relay, first, yc, 1, zh), (own, first, tz),
+            (y_end, 1, 1 - zh, 1), (gs_task, 1 - zh, 1), (xc, 0), (xa, 1), (xb, 1), (x_end, 3), (gf_task, 3),
+            (own, 1 - first, ya, 0, 1 - zh), (relay, 1 - first, yb, 0, 1 - zh), (own, 1 - first, ya, 1, zh),
+            (x_got, 0), (z_end, 0), (relay, 1 - first, yc, 0, 1 - zh), (relay, 1 - first, yb, 1, zh),
+            (xc, 1), (xb, 2), (xc, 2), (xa, 3), (xb, 3), (relay, 1 - first, yc, 1, zh),
+            (own, 1 - first, tz), (x_got, 1), (z_end, 1), (x_got, 2), (z_end, 2), (xc, 3),
+            (gf_end,), (gf_out,),
             (x_got, 3), (gs_out, 0), (gs_out, 1),
         )
         finish(0)
@@ -314,19 +318,18 @@
     def _():
         side[0] = 1
         run(
-            (zh_send,), (x_fwd, 0), (z_step, 1, 0), (z_step, 2, 0), (y_fwd, 0, zh), (z_step, 1, 1), (z_step, 2, 1),
-            (x_end, 0), (g_got,), (gf_task, 0), (z_step, 3, 0), (zh_got, 0), (z_step, 3, 1), (zh_got, 1), (x_fwd, 1),
-            (y_end, 0, zh), (gs_task, early), (x_fwd, 2), (y_fwd, 1, 1 - zh), (x_end, 1), (gf_task, 1),
-            (own, first, ya, 0, 1 - zh), (relay, first, yb, 0, 1 - zh), (own, first, ya, 1, zh), (gs_task, early + 1),
-            (x_fwd, 3), (y_end, 1, 1 - zh), (gs_task, late + odd), (xa, 0), (relay, first, yc, 0, 1 - zh), (gs_task, late + 1 - odd), (xb, 0),
-            (xa, 1), (relay, first, yb, 1, zh), (relay, first, yc, 1, zh),
-            (x_end, 2), (gf_task, 2), (xc, 0), (xb, 1), (xa, 2),
+            (zh_send, 0), (x_fwd, 0), (z_step, 1, 0), (y_fwd, 0, zh, 0), (y_fwd, 0, zh, 1), (z_step, 1, 1), (z_step, 2, 0), (z_step, 2, 1),
+            (x_end, 0), (g_got,), (gf_task, 0), (zh_got, 0), (z_step, 3, 0, 0), (z_step, 3, 1, 0), (x_fwd, 1), (x_out, 3, 0), (x_out, 3, 1), (zh_send, 1),
+            (y_end, 0, zh, 0), (gs_task, zh, 0), (y_fwd, 1, 1 - zh, 0), (x_fwd, 2), (y_end, 0, zh, 1), (gs_task, zh, 1),
+            (x_end, 1), (gf_task, 1), (own, first, ya, 0, 1 - zh), (relay, first, yb, 0, 1 - zh), (own, first, ya, 1, zh),
+            (zh_got, 1), (x_fwd, 3), (y_end, 1, 1 - zh, 0), (gs_task, 1 - zh, 0), (xa, 0), (xb, 0), (xa, 3),
+            (relay, first, yc, 0, 1 - zh), (y_fwd, 1, 1 - zh, 1), (relay, first, yb, 1, zh), (x_end, 2), (gf_task, 2), (relay, first, yc, 1, zh),
             (x_end, 3), (gf_task, 3), (own, 1 - first, ya, 0, 1 - zh), (relay, 1 - first, yb, 0, 1 - zh), (own, 1 - first, ya, 1, zh),
-            (own, first, tz),
-            (xc, 1), (xb, 2), (xa, 3), (x_got, 0),
-            (relay, 1 - first, yc, 0, 1 - zh), (relay, 1 - first, yb, 1, zh), (relay, 1 - first, yc, 1, zh), (xc, 2), (xb, 3),
-            (z_mid, 0, 0), (z_mid, 0, 1), (own, 1 - first, tz), (xc, 3), (x_got, 1),
-            (z_mid, 1, 0), (z_mid, 1, 1), (x_got, 2), (z_mid, 2, 0), (z_mid, 2, 1), (gf_end,), (gf_out,),
+            (xc, 0), (own, first, tz), (y_end, 1, 1 - zh, 1), (gs_task, 1 - zh, 1), (xa, 2), (xb, 2), (xa, 1),
+            (relay, 1 - first, yc, 0, 1 - zh), (relay, 1 - first, yb, 1, zh), (relay, 1 - first, yc, 1, zh),
+            (xc, 2), (xb, 1), (x_got, 0), (own, 1 - first, tz), (xc, 1), (xb, 3), (xc, 3),
+            (z_mid, 0, 0), (z_mid, 0, 1), (x_got, 2), (z_mid, 2, 0), (z_mid, 2, 1), (x_got, 1), (z_mid, 1, 0), (z_mid, 1, 1),
+            (gf_end,), (gf_out,),
             (x_got, 3), (gs_out, 0), (gs_out, 1),
         )
         finish(1)

time: 74.8 us -> 71.1 us (0.951)
  the two profiles are of different devices: /device:TPU:8 before, /device:TPU:32 now
where the time goes in v3:
time: 71.1 us; the launch traced here: 71 us
  Pallas kernels  69 us (97%)
  local copies, waits for them, and re-layouts  1.36 us (2%)
    pallas_call x1, Pallas kernels, local(): pl.pallas_call(kernel, out_shape=(jax.ShapeDtypeStruct((2, 2, 48, 512), B...  69 us

profile of v3, /device:TPU:32, one launch (start us, length us, event | category | flops | bytes accessed | tf_op | source)
XLA Modules:
  0.0 71.0 jit_solution(13188547869811220270)
XLA Ops:
  0.6 69.0 %shard_map.50 = (bf16[2,2,48,512]{3,2,1,0:T(8,128)(2,1)S(1)}, bf16[48,2048]{1,0:T(8,128)(2,1)S(1)}) custom-call(bf16[2,2,48,512]{3,2,1,0:T(8,128)(2,1)} %bitcast.3, bf16[48,2048]{1,0:T(8,128)(2,1)} %e2_hbm.1, f32[512,2048]{1,0:T(8,128)} %g_hbm.1), custom_call_target="tpu_custom_call" | custom-call | tf_op jit(solution)/shard_map/pallas_call | solution.py:342
  69.6 0.7 copy.7
  70.3 0.7 copy.8

commit v4 on v3

--- a/solution.py
+++ b/solution.py
@@ -60,8 +60,6 @@
     l1.start()
     l1own.start()
     lg = [pltpu.make_async_copy(g_hbm.at[pl.ds(i * 128, 128)], gst.at[i], gsem.at[i]) for i in range(4)]
-    for cp in lg:
-        cp.start()
 
     barrier = pltpu.get_barrier_semaphore()
     for d in (d_core, d_xp, d_xm, d_yp, d_ym, d_zh, d_in):
@@ -122,6 +120,8 @@
 
     l1.wait()
     go(e1s.at[:, 1 - c], E1.at[col, :, c], cs, (0,), cr.at[0], d_core)
+    for cp in lg:
+        cp.start()
     l1own.wait()
     got(E1.at[col, :, 1 - c], cr.at[0])
 
@@ -154,10 +154,12 @@
         y_send(1, 1 - zh, 0, h)
         y_send(1, 1 - zh, 1, h)
 
-    for i in range(4):
-        lg[i].wait()
-        G[c, pl.ds(i * 128, 128), :] = gst[i].astype(BF)
-        go(G.at[c, pl.ds(i * 128, 128)], G.at[c, pl.ds(i * 128, 128)], cs, (1 + i,), cr.at[1 + i], d_core)
+    def g_share():
+        for i in range(4):
+            lg[i].wait()
+            b = G.at[c, pl.ds(i * 128, 128)]
+            G[c, pl.ds(i * 128, 128), :] = gst[i].astype(BF)
+            go(b, b, cs, (1 + i,), cr.at[1 + i], d_core)
 
     def g_got():
         for i in range(4):
@@ -298,17 +300,17 @@
     def _():
         side[0] = 0
         run(
-            (zh_send, 0), (x_fwd, 0), (z_step, 1, 0), (y_fwd, 0, zh, 0), (y_fwd, 0, zh, 1), (z_step, 1, 1), (zh_got, 0),
+            (zh_send, 0), (g_share,), (x_fwd, 0), (z_step, 1, 0), (y_fwd, 0, zh, 0), (y_fwd, 0, zh, 1), (z_step, 1, 1), (zh_got, 0),
             (x_end, 0), (g_got,), (gf_task, 0), (x_fwd, 1), (z_step, 2, 0), (y_end, 0, zh, 0), (gs_task, zh, 0), (z_step, 2, 1), (zh_send, 1),
-            (y_fwd, 1, 1 - zh, 0), (x_end, 1), (gf_task, 1), (own, first, ya, 0, 1 - zh), (relay, first, yb, 0, 1 - zh), (own, first, ya, 1, zh),
-            (z_step, 3, 0), (x_fwd, 2), (z_step, 3, 1), (zh_got, 1), (y_end, 1, 1 - zh, 0), (gs_task, 1 - zh, 0), (xa, 0),
-            (relay, first, yc, 0, 1 - zh), (y_end, 0, zh, 1), (gs_task, zh, 1), (y_fwd, 1, 1 - zh, 1), (relay, first, yb, 1, zh),
-            (x_end, 2), (gf_task, 2), (x_fwd, 3), (xb, 0), (xa, 2), (relay, first, yc, 1, zh), (own, first, tz),
-            (y_end, 1, 1 - zh, 1), (gs_task, 1 - zh, 1), (xc, 0), (xa, 1), (xb, 1), (x_end, 3), (gf_task, 3),
-            (own, 1 - first, ya, 0, 1 - zh), (relay, 1 - first, yb, 0, 1 - zh), (own, 1 - first, ya, 1, zh),
-            (x_got, 0), (z_end, 0), (relay, 1 - first, yc, 0, 1 - zh), (relay, 1 - first, yb, 1, zh),
-            (xc, 1), (xb, 2), (xc, 2), (xa, 3), (xb, 3), (relay, 1 - first, yc, 1, zh),
-            (own, 1 - first, tz), (x_got, 1), (z_end, 1), (x_got, 2), (z_end, 2), (xc, 3),
+            (y_fwd, 1, 1 - zh, 0), (z_step, 3, 0), (x_end, 1), (gf_task, 1), (own, first, ya, 0, 1 - zh), (relay, first, yb, 0, 1 - zh),
+            (z_step, 3, 1), (zh_got, 1), (x_fwd, 2), (y_end, 1, 1 - zh, 0), (gs_task, 1 - zh, 0), (xa, 0),
+            (relay, first, yc, 0, 1 - zh), (y_end, 0, zh, 1), (gs_task, zh, 1), (x_fwd, 3), (xb, 0), (y_fwd, 1, 1 - zh, 1),
+            (x_end, 2), (gf_task, 2), (own, first, tz), (xc, 0),
+            (y_end, 1, 1 - zh, 1), (gs_task, 1 - zh, 1), (xa, 1), (xb, 1), (xa, 2), (x_end, 3), (gf_task, 3),
+            (own, 1 - first, ya, 0, 1 - zh), (relay, 1 - first, yb, 0, 1 - zh), (own, first, ya, 1, zh), (relay, first, yb, 1, zh),
+            (x_got, 0), (z_end, 0), (xc, 1), (xb, 2), (relay, 1 - first, yc, 0, 1 - zh), (relay, first, yc, 1, zh),
+            (own, 1 - first, ya, 1, zh), (relay, 1 - first, yb, 1, zh), (xc, 2), (xa, 3), (xb, 3), (own, 1 - first, tz),
+            (x_got, 1), (z_end, 1), (relay, 1 - first, yc, 1, zh), (x_got, 2), (z_end, 2), (xc, 3),
             (gf_end,), (gf_out,),
             (x_got, 3), (gs_out, 0), (gs_out, 1),
         )
@@ -318,17 +320,17 @@
     def _():
         side[0] = 1
         run(
-            (zh_send, 0), (x_fwd, 0), (z_step, 1, 0), (y_fwd, 0, zh, 0), (y_fwd, 0, zh, 1), (z_step, 1, 1), (z_step, 2, 0), (z_step, 2, 1),
+            (zh_send, 0), (g_share,), (x_fwd, 0), (z_step, 1, 0), (y_fwd, 0, zh, 0), (y_fwd, 0, zh, 1), (z_step, 1, 1), (z_step, 2, 0), (z_step, 2, 1),
             (x_end, 0), (g_got,), (gf_task, 0), (zh_got, 0), (z_step, 3, 0, 0), (z_step, 3, 1, 0), (x_fwd, 1), (x_out, 3, 0), (x_out, 3, 1), (zh_send, 1),
             (y_end, 0, zh, 0), (gs_task, zh, 0), (y_fwd, 1, 1 - zh, 0), (x_fwd, 2), (y_end, 0, zh, 1), (gs_task, zh, 1),
-            (x_end, 1), (gf_task, 1), (own, first, ya, 0, 1 - zh), (relay, first, yb, 0, 1 - zh), (own, first, ya, 1, zh),
-            (zh_got, 1), (x_fwd, 3), (y_end, 1, 1 - zh, 0), (gs_task, 1 - zh, 0), (xa, 0), (xb, 0), (xa, 3),
-            (relay, first, yc, 0, 1 - zh), (y_fwd, 1, 1 - zh, 1), (relay, first, yb, 1, zh), (x_end, 2), (gf_task, 2), (relay, first, yc, 1, zh),
-            (x_end, 3), (gf_task, 3), (own, 1 - first, ya, 0, 1 - zh), (relay, 1 - first, yb, 0, 1 - zh), (own, 1 - first, ya, 1, zh),
-            (xc, 0), (own, first, tz), (y_end, 1, 1 - zh, 1), (gs_task, 1 - zh, 1), (xa, 2), (xb, 2), (xa, 1),
-            (relay, 1 - first, yc, 0, 1 - zh), (relay, 1 - first, yb, 1, zh), (relay, 1 - first, yc, 1, zh),
-            (xc, 2), (xb, 1), (x_got, 0), (own, 1 - first, tz), (xc, 1), (xb, 3), (xc, 3),
-            (z_mid, 0, 0), (z_mid, 0, 1), (x_got, 2), (z_mid, 2, 0), (z_mid, 2, 1), (x_got, 1), (z_mid, 1, 0), (z_mid, 1, 1),
+            (x_end, 1), (gf_task, 1), (own, first, ya, 0, 1 - zh), (relay, first, yb, 0, 1 - zh),
+            (zh_got, 1), (x_fwd, 3), (y_end, 1, 1 - zh, 0), (gs_task, 1 - zh, 0), (xa, 0), (xb, 0), (xa, 3), (xb, 3),
+            (relay, first, yc, 0, 1 - zh), (y_fwd, 1, 1 - zh, 1), (x_end, 2), (gf_task, 2), (xc, 0), (own, first, tz),
+            (y_end, 1, 1 - zh, 1), (gs_task, 1 - zh, 1), (xa, 2), (xb, 2), (xa, 1),
+            (x_end, 3), (gf_task, 3), (own, 1 - first, ya, 0, 1 - zh), (relay, 1 - first, yb, 0, 1 - zh), (own, first, ya, 1, zh), (relay, first, yb, 1, zh),
+            (relay, 1 - first, yc, 0, 1 - zh), (xc, 2), (xb, 1), (x_got, 0), (z_mid, 0, 0), (relay, first, yc, 1, zh), (own, 1 - first, ya, 1, zh), (relay, 1 - first, yb, 1, zh),
+            (own, 1 - first, tz), (z_mid, 0, 1), (xc, 1), (xc, 3),
+            (x_got, 2), (z_mid, 2, 0), (relay, 1 - first, yc, 1, zh), (z_mid, 2, 1), (x_got, 1), (z_mid, 1, 0), (z_mid, 1, 1),
             (gf_end,), (gf_out,),
             (x_got, 3), (gs_out, 0), (gs_out, 1),
         )

time: 71.1 us -> 69.3 us (0.975)
  Pallas kernels: 69 us -> 67.2 us
    pallas_call x1, Pallas kernels: 69 us -> 67.2 us  [local(): pl.pallas_call(kernel, out_shape=(jax.ShapeDtypeStruct((2, 2, 48, 512), B...]
where the time goes in v4:
time: 69.3 us; the launch traced here: 69.2 us
  Pallas kernels  67.2 us (97%)
  local copies, waits for them, and re-layouts  1.36 us (2%)
    pallas_call x1, Pallas kernels, local(): pl.pallas_call(kernel, out_shape=(jax.ShapeDtypeStruct((2, 2, 48, 512), B...  67.2 us

profile of v4, /device:TPU:32, one launch (start us, length us, event | category | flops | bytes accessed | tf_op | source)
XLA Modules:
  0.0 69.2 jit_solution(5479925614931014182)
XLA Ops:
  0.6 67.2 %shard_map.50 = (bf16[2,2,48,512]{3,2,1,0:T(8,128)(2,1)S(1)}, bf16[48,2048]{1,0:T(8,128)(2,1)S(1)}) custom-call(bf16[2,2,48,512]{3,2,1,0:T(8,128)(2,1)} %bitcast.3, bf16[48,2048]{1,0:T(8,128)(2,1)} %e2_hbm.1, f32[512,2048]{1,0:T(8,128)} %g_hbm.1), custom_call_target="tpu_custom_call" | custom-call | tf_op jit(solution)/shard_map/pallas_call | solution.py:344
  67.9 0.7 copy.7
  68.5 0.7 copy.8

commit v5 on v4

--- a/solution.py
+++ b/solution.py
@@ -305,11 +305,11 @@
             (y_fwd, 1, 1 - zh, 0), (z_step, 3, 0), (x_end, 1), (gf_task, 1), (own, first, ya, 0, 1 - zh), (relay, first, yb, 0, 1 - zh),
             (z_step, 3, 1), (zh_got, 1), (x_fwd, 2), (y_end, 1, 1 - zh, 0), (gs_task, 1 - zh, 0), (xa, 0),
             (relay, first, yc, 0, 1 - zh), (y_end, 0, zh, 1), (gs_task, zh, 1), (x_fwd, 3), (xb, 0), (y_fwd, 1, 1 - zh, 1),
-            (x_end, 2), (gf_task, 2), (own, first, tz), (xc, 0),
+            (own, first, tz), (x_end, 2), (gf_task, 2), (xc, 0),
             (y_end, 1, 1 - zh, 1), (gs_task, 1 - zh, 1), (xa, 1), (xb, 1), (xa, 2), (x_end, 3), (gf_task, 3),
             (own, 1 - first, ya, 0, 1 - zh), (relay, 1 - first, yb, 0, 1 - zh), (own, first, ya, 1, zh), (relay, first, yb, 1, zh),
-            (x_got, 0), (z_end, 0), (xc, 1), (xb, 2), (relay, 1 - first, yc, 0, 1 - zh), (relay, first, yc, 1, zh),
-            (own, 1 - first, ya, 1, zh), (relay, 1 - first, yb, 1, zh), (xc, 2), (xa, 3), (xb, 3), (own, 1 - first, tz),
+            (x_got, 0), (z_end, 0), (relay, 1 - first, yc, 0, 1 - zh), (xc, 1), (xb, 2), (relay, first, yc, 1, zh),
+            (own, 1 - first, ya, 1, zh), (relay, 1 - first, yb, 1, zh), (own, 1 - first, tz), (xc, 2), (xa, 3), (xb, 3),
             (x_got, 1), (z_end, 1), (relay, 1 - first, yc, 1, zh), (x_got, 2), (z_end, 2), (xc, 3),
             (gf_end,), (gf_out,),
             (x_got, 3), (gs_out, 0), (gs_out, 1),
@@ -325,11 +325,11 @@
             (y_end, 0, zh, 0), (gs_task, zh, 0), (y_fwd, 1, 1 - zh, 0), (x_fwd, 2), (y_end, 0, zh, 1), (gs_task, zh, 1),
             (x_end, 1), (gf_task, 1), (own, first, ya, 0, 1 - zh), (relay, first, yb, 0, 1 - zh),
             (zh_got, 1), (x_fwd, 3), (y_end, 1, 1 - zh, 0), (gs_task, 1 - zh, 0), (xa, 0), (xb, 0), (xa, 3), (xb, 3),
-            (relay, first, yc, 0, 1 - zh), (y_fwd, 1, 1 - zh, 1), (x_end, 2), (gf_task, 2), (xc, 0), (own, first, tz),
-            (y_end, 1, 1 - zh, 1), (gs_task, 1 - zh, 1), (xa, 2), (xb, 2), (xa, 1),
-            (x_end, 3), (gf_task, 3), (own, 1 - first, ya, 0, 1 - zh), (relay, 1 - first, yb, 0, 1 - zh), (own, first, ya, 1, zh), (relay, first, yb, 1, zh),
-            (relay, 1 - first, yc, 0, 1 - zh), (xc, 2), (xb, 1), (x_got, 0), (z_mid, 0, 0), (relay, first, yc, 1, zh), (own, 1 - first, ya, 1, zh), (relay, 1 - first, yb, 1, zh),
-            (own, 1 - first, tz), (z_mid, 0, 1), (xc, 1), (xc, 3),
+            (relay, first, yc, 0, 1 - zh), (y_fwd, 1, 1 - zh, 1), (x_end, 2), (gf_task, 2), (own, first, tz), (x_end, 3), (gf_task, 3),
+            (own, 1 - first, ya, 0, 1 - zh), (relay, 1 - first, yb, 0, 1 - zh), (xc, 0),
+            (y_end, 1, 1 - zh, 1), (gs_task, 1 - zh, 1), (xa, 2), (xb, 2), (xa, 1), (own, first, ya, 1, zh), (relay, first, yb, 1, zh),
+            (relay, 1 - first, yc, 0, 1 - zh), (relay, first, yc, 1, zh), (own, 1 - first, ya, 1, zh), (relay, 1 - first, yb, 1, zh),
+            (x_got, 0), (own, 1 - first, tz), (z_mid, 0, 0), (xc, 2), (xb, 1), (z_mid, 0, 1), (xc, 1), (xc, 3),
             (x_got, 2), (z_mid, 2, 0), (relay, 1 - first, yc, 1, zh), (z_mid, 2, 1), (x_got, 1), (z_mid, 1, 0), (z_mid, 1, 1),
             (gf_end,), (gf_out,),
             (x_got, 3), (gs_out, 0), (gs_out, 1),

time: 69.3 us -> 68.7 us (level)
  no operation moved by 1% of the time
where the time goes in v5:
time: 68.7 us; the launch traced here: 68.6 us
  Pallas kernels  66.6 us (97%)
  local copies, waits for them, and re-layouts  1.36 us (2%)
    pallas_call x1, Pallas kernels, local(): pl.pallas_call(kernel, out_shape=(jax.ShapeDtypeStruct((2, 2, 48, 512), B...  66.6 us

profile of v5, /device:TPU:32, one launch (start us, length us, event | category | flops | bytes accessed | tf_op | source)
XLA Modules:
  0.0 68.6 jit_solution(14203925893133980084)
XLA Ops:
  0.6 66.6 %shard_map.50 = (bf16[2,2,48,512]{3,2,1,0:T(8,128)(2,1)S(1)}, bf16[48,2048]{1,0:T(8,128)(2,1)S(1)}) custom-call(bf16[2,2,48,512]{3,2,1,0:T(8,128)(2,1)} %bitcast.3, bf16[48,2048]{1,0:T(8,128)(2,1)} %e2_hbm.1, f32[512,2048]{1,0:T(8,128)} %g_hbm.1), custom_call_target="tpu_custom_call" | custom-call | tf_op jit(solution)/shard_map/pallas_call | solution.py:344
  67.2 0.7 copy.7
  67.9 0.7 copy.8

commit v6 on v5

--- a/solution.py
+++ b/solution.py
@@ -141,8 +141,12 @@
         got(E1.at[q * 4 + (yp, ym)[h], half[h]], yr.at[i, 1 - h, h])
         got(E1.at[q * 4 + yo, half[h]], yr.at[i, 2, h])
 
-    for r, h in ((0, 0), (1, 1), (0, 1), (1, 0)):
-        y_send(0, zh, r, h)
+    for r in range(2):
+        y_send(0, zh, r, 0)
+
+    def y_rest():
+        for r in range(2):
+            y_send(0, zh, r, 1)
 
     def zh_send(*hs):
         for h in hs:
@@ -300,8 +304,8 @@
     def _():
         side[0] = 0
         run(
-            (zh_send, 0), (g_share,), (x_fwd, 0), (z_step, 1, 0), (y_fwd, 0, zh, 0), (y_fwd, 0, zh, 1), (z_step, 1, 1), (zh_got, 0),
-            (x_end, 0), (g_got,), (gf_task, 0), (x_fwd, 1), (z_step, 2, 0), (y_end, 0, zh, 0), (gs_task, zh, 0), (z_step, 2, 1), (zh_send, 1),
+            (zh_send, 0), (g_share,), (x_fwd, 0), (z_step, 1, 0), (y_rest,), (y_fwd, 0, zh, 0), (z_step, 1, 1), (zh_got, 0),
+            (x_end, 0), (g_got,), (gf_task, 0), (x_fwd, 1), (z_step, 2, 0), (y_fwd, 0, zh, 1), (y_end, 0, zh, 0), (gs_task, zh, 0), (z_step, 2, 1), (zh_send, 1),
             (y_fwd, 1, 1 - zh, 0), (z_step, 3, 0), (x_end, 1), (gf_task, 1), (own, first, ya, 0, 1 - zh), (relay, first, yb, 0, 1 - zh),
             (z_step, 3, 1), (zh_got, 1), (x_fwd, 2), (y_end, 1, 1 - zh, 0), (gs_task, 1 - zh, 0), (xa, 0),
             (relay, first, yc, 0, 1 - zh), (y_end, 0, zh, 1), (gs_task, zh, 1), (x_fwd, 3), (xb, 0), (y_fwd, 1, 1 - zh, 1),
@@ -320,16 +324,16 @@
     def _():
         side[0] = 1
         run(
-            (zh_send, 0), (g_share,), (x_fwd, 0), (z_step, 1, 0), (y_fwd, 0, zh, 0), (y_fwd, 0, zh, 1), (z_step, 1, 1), (z_step, 2, 0), (z_step, 2, 1),
-            (x_end, 0), (g_got,), (gf_task, 0), (zh_got, 0), (z_step, 3, 0, 0), (z_step, 3, 1, 0), (x_fwd, 1), (x_out, 3, 0), (x_out, 3, 1), (zh_send, 1),
+            (zh_send, 0), (g_share,), (x_fwd, 0), (z_step, 1, 0), (y_rest,), (y_fwd, 0, zh, 0), (z_step, 1, 1), (z_step, 2, 0), (z_step, 2, 1),
+            (x_end, 0), (g_got,), (gf_task, 0), (y_fwd, 0, zh, 1), (zh_got, 0), (z_step, 3, 0, 0), (z_step, 3, 1, 0), (x_fwd, 1), (x_out, 3, 0), (x_out, 3, 1), (zh_send, 1),
             (y_end, 0, zh, 0), (gs_task, zh, 0), (y_fwd, 1, 1 - zh, 0), (x_fwd, 2), (y_end, 0, zh, 1), (gs_task, zh, 1),
             (x_end, 1), (gf_task, 1), (own, first, ya, 0, 1 - zh), (relay, first, yb, 0, 1 - zh),
-            (zh_got, 1), (x_fwd, 3), (y_end, 1, 1 - zh, 0), (gs_task, 1 - zh, 0), (xa, 0), (xb, 0), (xa, 3), (xb, 3),
+            (zh_got, 1), (x_fwd, 3), (y_end, 1, 1 - zh, 0), (gs_task, 1 - zh, 0), (xa, 0), (xb, 0), (xa, 3),
             (relay, first, yc, 0, 1 - zh), (y_fwd, 1, 1 - zh, 1), (x_end, 2), (gf_task, 2), (own, first, tz), (x_end, 3), (gf_task, 3),
             (own, 1 - first, ya, 0, 1 - zh), (relay, 1 - first, yb, 0, 1 - zh), (xc, 0),
             (y_end, 1, 1 - zh, 1), (gs_task, 1 - zh, 1), (xa, 2), (xb, 2), (xa, 1), (own, first, ya, 1, zh), (relay, first, yb, 1, zh),
             (relay, 1 - first, yc, 0, 1 - zh), (relay, first, yc, 1, zh), (own, 1 - first, ya, 1, zh), (relay, 1 - first, yb, 1, zh),
-            (x_got, 0), (own, 1 - first, tz), (z_mid, 0, 0), (xc, 2), (xb, 1), (z_mid, 0, 1), (xc, 1), (xc, 3),
+            (x_got, 0), (own, 1 - first, tz), (z_mid, 0, 0), (xc, 2), (xb, 1), (z_mid, 0, 1), (xc, 1), (xb, 3), (xc, 3),
             (x_got, 2), (z_mid, 2, 0), (relay, 1 - first, yc, 1, zh), (z_mid, 2, 1), (x_got, 1), (z_mid, 1, 0), (z_mid, 1, 1),
             (gf_end,), (gf_out,),
             (x_got, 3), (gs_out, 0), (gs_out, 1),

time: 68.7 us -> 68.6 us (level)
  no operation moved by 1% of the time
where the time goes in v6:
time: 68.6 us; the launch traced here: 68.5 us
  Pallas kernels  66.5 us (97%)
  local copies, waits for them, and re-layouts  1.36 us (2%)
    pallas_call x1, Pallas kernels, local(): pl.pallas_call(kernel, out_shape=(jax.ShapeDtypeStruct((2, 2, 48, 512), B...  66.5 us

profile of v6, /device:TPU:32, one launch (start us, length us, event | category | flops | bytes accessed | tf_op | source)
XLA Modules:
  0.0 68.5 jit_solution(4998383817719737369)
XLA Ops:
  0.6 66.5 %shard_map.50 = (bf16[2,2,48,512]{3,2,1,0:T(8,128)(2,1)S(1)}, bf16[48,2048]{1,0:T(8,128)(2,1)S(1)}) custom-call(bf16[2,2,48,512]{3,2,1,0:T(8,128)(2,1)} %bitcast.3, bf16[48,2048]{1,0:T(8,128)(2,1)} %e2_hbm.1, f32[512,2048]{1,0:T(8,128)} %g_hbm.1), custom_call_target="tpu_custom_call" | custom-call | tf_op jit(solution)/shard_map/pallas_call | solution.py:348
  67.1 0.7 copy.7
  67.8 0.7 copy.8
